TPU v7x, 32 devices: a whole 2x2x4 slice. The times are simulated.
32 devices in a mesh: groups: 2 (over x), patch: 16 (over z, y, core).
Axes of the slice: x: 2, y: 2, z: 4, core: 2. Of those that a mesh axis runs over, the one named last changes fastest.
Arguments:
- tokens: bfloat16 [16384, 1152], P(('groups', 'patch')), parts along dimension 0, may hold values from -6 to 6
- stale_kv: bfloat16 [16384, 1152], P(('groups', 'patch')), parts along dimension 0, may hold values from -40 to 40, as said below
- mod_table: float32 [6, 1152], replicated, may hold values from -2 to 3
- mod_mix: float32 [6, 1152], replicated, may hold values from -3 to 3
- timestep: int32 [2], P('groups'), parts along dimension 0, may hold values from 0 to 999
- frame_order: int32 [8], P('groups'), parts along dimension 0, may hold values from 0 to 3, each once
- spatial_qkv: bfloat16 [3, 1152, 576], replicated, may hold values from -0.1875 to 0.1875
- spatial_out: bfloat16 [576, 1152], replicated, may hold values from -0.25 to 0.25
- temporal_qkv: bfloat16 [3, 1152, 576], replicated, may hold values from -0.1875 to 0.1875
- temporal_out: bfloat16 [576, 1152], replicated, may hold values from -0.25 to 0.25
Outputs:
- block_out: float32 [16384, 1152], P(('groups', 'patch')), parts along dimension 0
There are 2 independent parts, one for each index of `groups`. A program takes and returns all parts, laid end to end along the dimension named above; an argument that names none is the same for every part. Nothing has to cross between parts.
Inputs may be any that keep to these rules, and one draw needn't show every extreme that they name: `frame_order`: a permutation of the 4 time positions. `stale_kv`: previous step's keys and values.
All inputs are finite; a program needn't handle non-finite values.
Results may differ from a plain program's by a relative error of at most 0.013.
The roundings to bfloat16 on the way count: a program that leaves them out, or rounds other values in their place, can miss the bound.
Values may be sent and summed in bfloat16 or wider, within the bound.
A program may use at most 128 MiB of HBM per device.

v0:
```python
import math

import jax
import jax.numpy as jnp
from jax import lax
from jax.sharding import PartitionSpec as P

HEADS = 16


epsilon = 1e-06


def from_partner(value, axis, distance):
    mask = 2**distance
    pairs = [(source, source ^ mask) for source in range(lax.axis_size(axis))]
    return lax.ppermute(value, axis, pairs)


def normalize(activations):
    row_mean = jnp.mean(activations, axis=-1, keepdims=True)
    centered = activations - row_mean
    variance = jnp.mean(centered * centered, axis=-1, keepdims=True)
    return centered * lax.rsqrt(variance + epsilon)


def sinusoid(position, feature_width):
    half_width = feature_width // 2
    frequencies = jnp.exp(
        -math.log(10000.0) * jnp.arange(half_width, dtype=jnp.float32) / half_width
    )
    angles = jnp.asarray(position).astype(jnp.float32)[..., None] * frequencies
    return jnp.concatenate([jnp.sin(angles), jnp.cos(angles)], axis=-1)


def softmax_rows(scores):
    row_top = jnp.max(scores, axis=-1, keepdims=True)
    exp_scores = jnp.exp(scores - row_top)
    return (exp_scores / jnp.sum(exp_scores, axis=-1, keepdims=True)).astype(jnp.bfloat16)


def spatial_attend(queries, key_rows, value_rows, head_dim):
    width_win = queries.shape[1]
    head_count = width_win // head_dim
    query_heads = queries.reshape(-1, head_count, head_dim)
    key_heads = key_rows.reshape(-1, head_count, head_dim)
    value_heads = value_rows.reshape(-1, head_count, head_dim)
    scores = jnp.einsum(
        "qhe,khe->hqk", query_heads, key_heads, preferred_element_type=jnp.float32
    ) * head_dim ** (-0.5)
    weights = softmax_rows(scores)
    mixed_out = jnp.einsum("hqk,khe->qhe", weights, value_heads, preferred_element_type=jnp.float32)
    return mixed_out.reshape(-1, width_win).astype(jnp.bfloat16)


def temporal_attend(queries, key_rows, value_rows, head_dim):
    frame_count, pixel_count, width_win = queries.shape
    head_count = width_win // head_dim
    shape_heads = (frame_count, pixel_count, head_count, head_dim)
    query_heads = queries.reshape(shape_heads)
    key_heads = key_rows.reshape(shape_heads)
    value_heads = value_rows.reshape(shape_heads)
    scores = jnp.einsum(
        "fmhe,gmhe->mhfg", query_heads, key_heads, preferred_element_type=jnp.float32
    ) * head_dim ** (-0.5)
    weights = softmax_rows(scores)
    mixed_out = jnp.einsum(
        "mhfg,gmhe->fmhe", weights, value_heads, preferred_element_type=jnp.float32
    )
    return mixed_out.reshape(frame_count, pixel_count, width_win).astype(jnp.bfloat16)


def per_device(
    tokens,
    stale_kv,
    mod_table,
    mod_mix,
    timestep,
    frame_order,
    spatial_qkv,
    spatial_out,
    temporal_qkv,
    temporal_out,
):
    devices = lax.axis_size("patch")
    dev_index = lax.axis_index("patch")
    frames = devices // 4
    quarter = dev_index % 4
    frame_slot = dev_index // 4
    row_count, feature_width = tokens.shape
    width_win = spatial_out.shape[0]
    head_dim = feature_width // HEADS
    modulation = mod_table + mod_mix * sinusoid(timestep[0], feature_width)[None, :]
    tokens_wide = tokens.astype(jnp.float32)
    spatial_in = (normalize(tokens_wide) * (1.0 + modulation[1]) + modulation[0]).astype(
        jnp.bfloat16
    )
    fresh_qkv = jnp.einsum(
        "tr,jrd->jtd", spatial_in, spatial_qkv, preferred_element_type=jnp.float32
    ).astype(jnp.bfloat16)
    bit_order = (0, 1)
    kv_block = stale_kv
    for bit_num in bit_order:
        partner = from_partner(kv_block, "patch", bit_num)
        low_half = dev_index >> bit_num & 1 == 0
        kv_block = jnp.where(
            low_half, jnp.stack([kv_block, partner], 0), jnp.stack([partner, kv_block], 0)
        )
    kv_block = kv_block.reshape(4, row_count, 2 * width_win)
    own_mask = (jnp.arange(4) == quarter)[:, None, None]
    key_rows = jnp.where(own_mask, fresh_qkv[1][None], kv_block[:, :, :width_win]).reshape(
        4 * row_count, width_win
    )
    value_rows = jnp.where(own_mask, fresh_qkv[2][None], kv_block[:, :, width_win:]).reshape(
        4 * row_count, width_win
    )
    spatial_mixed = spatial_attend(fresh_qkv[0], key_rows, value_rows, head_dim)
    spatial_proj = jnp.dot(spatial_mixed, spatial_out, preferred_element_type=jnp.float32)
    after_spatial = tokens_wide + modulation[2] * spatial_proj
    frame_id = jnp.sum(jnp.where(jnp.arange(frames) == frame_slot, frame_order, 0))
    temporal_in = (
        normalize(after_spatial) * (1.0 + modulation[4])
        + modulation[3]
        + sinusoid(frame_id, feature_width)[None, :]
    ).astype(jnp.bfloat16)
    piece_rows = row_count // devices
    arriving = lax.all_to_all(
        temporal_in.reshape(devices, piece_rows, feature_width),
        "patch",
        split_axis=0,
        concat_axis=0,
        tiled=True,
    )
    arranged = arriving.reshape(frames, 4 * piece_rows, feature_width)
    flat_rows = arranged.reshape(-1, feature_width)
    temporal_proj = jnp.einsum(
        "tr,jrd->jtd", flat_rows, temporal_qkv, preferred_element_type=jnp.float32
    )
    temporal_proj = temporal_proj.astype(jnp.bfloat16).reshape(
        (3,) + arranged.shape[:-1] + (width_win,)
    )
    mixed_out = temporal_attend(temporal_proj[0], temporal_proj[1], temporal_proj[2], head_dim)
    returning = lax.all_to_all(
        mixed_out.reshape(devices, piece_rows, width_win),
        "patch",
        split_axis=0,
        concat_axis=0,
        tiled=True,
    )
    temporal_mixed = returning.reshape(row_count, width_win)
    temporal_proj_out = jnp.dot(temporal_mixed, temporal_out, preferred_element_type=jnp.float32)
    return after_spatial + modulation[5] * temporal_proj_out


def solution(mesh):
    return jax.shard_map(
        per_device,
        mesh=mesh,
        in_specs=(
            P(("groups", "patch"), None),
            P(("groups", "patch"), None),
            P(),
            P(),
            P("groups"),
            P("groups"),
            P(),
            P(),
            P(),
            P(),
        ),
        out_specs=P(("groups", "patch"), None),
        check_vma=False,
    )
```

profile of v0, /device:TPU:0, one launch (start us, length us, event | category | flops | bytes accessed | tf_op | source)
XLA Modules:
  0.0 210.0 jit_solution(12419421594038518087)
XLA Ops:
  0.0 0.0 copy-start
  0.0 0.5 collective-permute-start
  1.2 0.1 pad_maximum_fusion
  1.3 1.5 convert_reduce_fusion
  2.8 0.8 multiply_add_fusion
  3.6 0.0 collective-permute-done
  3.6 0.0 copy-start.3
  3.6 3.9 %maximum_select_fusion.2 = bf16[2,512,1152]{2,1,0:T(8,128)(2,1)} fusion(bf16[1,512,1152]{2,1,0:T(8,128)(2,1)S(1)} %bitcast.59, bf16[1,512,1152]{2,1,0:T(8,128)(2,1)} %bitcast.57, pred[]{:T(512)S(6)} %eq.27), kind=kLoop, calls=%fused_computation.24 | loop fusion | flops 3538944 | bytes 4718593 | tf_op jit(solution)/shard_map/jit(_where)/select_n | solution.py:106
  7.5 0.0 copy-done.3
  7.5 2.6 %collective-permute-start.1 = (bf16[2,512,1152]{2,1,0:T(8,128)(2,1)}, bf16[2,512,1152]{2,1,0:T(8,128)(2,1)}, u32[]{:S(2)}, u32[]{:S(2)}) collective-permute-start(bf16[2,512,1152]{2,1,0:T(8,128)(2,1)} %maximum_select_fusion.2), channel_id=1, source_target_pairs={{0,2},{1,3},{2,0},{3,1},{4,6},{5,7},{6,4},{7,5},{8,10},{9,11},{10,... | collective-permute-start | bytes 7077896 | tf_op jit(solution)/shard_map/ppermute | solution.py:17
  10.1 0.6 slice_reduce_fusion.1
  10.7 1.7 fusion.10
  12.4 5.2 %convert_bitcast_fusion.1 = bf16[3,512,576]{1,2,0:T(8,128)(2,1)S(1)} fusion(bf16[3,1152,576]{1,2,0:T(8,128)(2,1)} %param.16, bf16[512,1152]{1,0:T(8,128)(2,1)} %param.10, f32[1152]{0:T(1024)S(1)} %get-tuple-element.8, f32[1152]{0:T(1024)S(1)} %get-tuple-element.9, f32[512]{0:T(512)S(1)} %add_rsqrt_fusion.1, f32[512]{0:T(512)S(1)} %broadcast_multiply_fusion.1), kind=kOutput, calls=%fused_computation.33 | convolution fusion | flops 2042855424 | bytes 6943744 | tf_op jit(solution)/shard_map/tr,jrd->jtd/dot_general | solution.py:98
  17.6 0.0 copy-start.11
  17.6 0.0 copy-start.2
  17.6 1.3 slice_bitcast_fusion
  18.9 1.4 copy.21
  20.3 2.2 %copy.19 = bf16[512,576]{1,0:T(8,128)(2,1)} copy(bf16[512,576]{0,1:T(8,128)(2,1)} %get-tuple-element.18) | data formatting | bytes 1179648 | tf_op jit(solution)/shard_map/jit(_where)/broadcast_in_dim | solution.py:114
  22.4 0.0 copy-done.11
  22.4 0.6 fusion.34
  23.7 0.1 fusion.32
  23.8 0.1 pad_maximum_fusion.1
  23.9 0.0 copy-done.2
  23.9 2.0 maximum_select_fusion.1
  25.9 36.3 %collective-permute-done.1 = bf16[2,512,1152]{2,1,0:T(8,128)(2,1)} collective-permute-done((bf16[2,512,1152]{2,1,0:T(8,128)(2,1)}, bf16[2,512,1152]{2,1,0:T(8,128)(2,1)}, u32[]{:S(2)}, u32[]{:S(2)}) %collective-permute-start.1) | collective-permute-done | bytes 2359328 | tf_op jit(solution)/shard_map/ppermute | solution.py:17
  62.2 0.0 copy-start.5
  62.2 3.1 %maximum_select_fusion = bf16[2,2,512,1152]{3,2,1,0:T(8,128)(2,1)S(1)} fusion(bf16[1,2,512,1152]{3,2,1,0:T(8,128)(2,1)} %bitcast.8, bf16[1,2,512,1152]{3,2,1,0:T(8,128)(2,1)S(1)} %maximum_select_fusion.1, pred[]{:T(512)S(6)} %eq.26), kind=kLoop, calls=%fused_computation.8 | loop fusion | flops 7077888 | bytes 9437185 | tf_op jit(solution)/shard_map/jit(_where)/select_n | solution.py:106
  65.3 0.0 copy-done.5
  65.3 3.4 %slice_select_fusion = (bf16[4,512,576]{2,1,0:T(8,128)(2,1)}, bf16[4,512,576]{2,1,0:T(8,128)(2,1)}) fusion(bf16[4,512,1152]{2,1,0:T(8,128)(2,1)S(1)} %bitcast.56, pred[4]{0:T(512)(128)(4,1)S(1)} %iota_compare_fusion, bf16[512,576]{1,0:T(8,128)(2,1)S(1)} %copy.21, bf16[512,576]{1,0:T(8,128)(2,1)S(1)} %copy-done.5), kind=kLoop, calls=%fused_computation.17 | loop fusion | flops 2359296 | bytes 10616836 | tf_op jit(solution)/shard_map/jit(_where)/select_n | solution.py:111
  68.7 5.4 %copy.20 = bf16[4,512,576]{1,0,2:T(4,128)(2,1)} copy(bf16[4,512,576]{2,1,0:T(8,128)(2,1)} %get-tuple-element.12) | data formatting | bytes 4718592 | tf_op jit(solution)/shard_map/jit(_where)/select_n | solution.py:114
  74.1 5.8 %reshape_reshape.9 = bf16[2048,8,72]{0,2,1:T(8,128)(2,1)} reshape(bf16[4,512,576]{1,0,2:T(4,128)(2,1)} %copy.20) | data formatting | bytes 4718592 | tf_op jit(solution)/shard_map/reshape;reshape | solution.py:47
  80.0 5.4 %copy.22 = bf16[4,512,576]{1,0,2:T(4,128)(2,1)} copy(bf16[4,512,576]{2,1,0:T(8,128)(2,1)} %get-tuple-element.11) | data formatting | bytes 4718592 | tf_op jit(solution)/shard_map/jit(_where)/select_n | solution.py:111
  85.4 0.0 copy-start.8
  85.4 5.9 %reshape_reshape.10 = bf16[2048,8,72]{0,2,1:T(8,128)(2,1)} reshape(bf16[4,512,576]{1,0,2:T(4,128)(2,1)} %copy.22) | data formatting | bytes 4718592 | tf_op jit(solution)/shard_map/reshape;reshape | solution.py:46
  91.4 0.0 copy-done.8
  91.4 17.3 %fusion.38 = (f32[8,512]{1,0:T(8,128)S(1)}, f32[8,512,2048]{2,1,0:T(8,128)}) fusion(bf16[512,8,72]{0,2,1:T(8,128)(2,1)S(1)} %bitcast.64, bf16[2048,8,72]{0,2,1:T(8,128)(2,1)} %reshape_reshape.10), kind=kOutput, calls=%fused_computation.73 | convolution fusion | flops 1233127424 | bytes 36519936 | tf_op jit(solution)/shard_map/sub | solution.py:38
  108.7 14.1 %fusion.18 = bf16[8,72,512]{2,1,0:T(8,128)(2,1)S(1)} fusion(bf16[2048,8,72]{0,2,1:T(8,128)(2,1)} %reshape_reshape.9, f32[8,512,2048]{2,1,0:T(8,128)} %get-tuple-element.20, f32[8,512]{1,0:T(8,128)S(1)} %get-tuple-element.19), kind=kOutput, calls=%fused_computation.36 | convolution fusion | flops 1225031680 | bytes 36519936 | tf_op jit(solution)/shard_map/hqk,khe->qhe/dot_general | solution.py:52
  122.8 0.0 copy-done
  122.8 0.0 copy-done.4
  122.8 1.4 fusion.39
  124.2 0.4 multiply_reduce_fusion.1
  124.6 0.0 copy-start.10
  124.6 0.5 add_convert_fusion
  125.2 0.5 copy-done.1
  125.6 35.6 %all_to_all.10 = bf16[16,32,1152]{2,1,0:T(8,128)(2,1)S(1)} all-to-all(bf16[16,32,1152]{2,1,0:T(8,128)(2,1)S(1)} %bitcast.61), channel_id=1, replica_groups=mesh['groups'=2,'patch'=16] {'patch'}, dimensions={0} | all-to-all | bytes 2359296 | tf_op jit(solution)/shard_map/all_to_all | solution.py:127
  161.2 0.0 copy-done.10
  161.2 2.5 %convert_bitcast_fusion = bf16[3,512,576]{1,2,0:T(8,128)(2,1)S(1)} fusion(bf16[512,1152,1]{1,0,2:T(8,128)(2,1)S(1)} %bitcast.63, bf16[3,1152,576]{1,2,0:T(8,128)(2,1)S(1)} %copy-done.10), kind=kOutput, calls=%fused_computation.32 | convolution fusion | flops 2039316480 | bytes 6930432 | tf_op jit(solution)/shard_map/tr,jrd->jtd/dot_general | solution.py:136
  163.8 0.1 fusion.37
  163.9 0.9 reshape_squeeze.13
  164.9 3.4 %copy.25 = bf16[4,128,8,72]{3,0,2,1:T(4,128)(2,1)} copy(bf16[4,128,8,72]{1,0,3,2:T(4,128)(2,1)} %reshape_squeeze.13) | data formatting | bytes 1179648 | tf_op jit(solution)/shard_map/reshape;squeeze | solution.py:62
  168.2 0.1 reshape_squeeze.14
  168.4 2.4 %copy.23 = bf16[4,128,8,72]{3,0,2,1:T(4,128)(2,1)} copy(bf16[4,128,8,72]{1,0,3,2:T(4,128)(2,1)S(1)} %reshape_squeeze.14) | data formatting | bytes 1179648 | tf_op jit(solution)/shard_map/reshape;squeeze | solution.py:60
  170.8 0.1 reshape_squeeze.15
  170.9 2.4 %copy.24 = bf16[4,128,8,72]{3,0,2,1:T(4,128)(2,1)} copy(bf16[4,128,8,72]{1,0,3,2:T(4,128)(2,1)S(1)} %reshape_squeeze.15) | data formatting | bytes 1179648 | tf_op jit(solution)/shard_map/reshape;squeeze | solution.py:61
  173.3 0.0 copy-done.7
  173.3 6.7 %fusion.40 = (f32[128,8,4]{2,1,0:T(8,128)}, f32[128,8,4,4]{2,3,1,0:T(4,128)}) fusion(bf16[4,128,8,72]{3,0,2,1:T(4,128)(2,1)S(1)} %copy-done.7, bf16[4,128,8,72]{3,0,2,1:T(4,128)(2,1)} %copy.24), kind=kOutput, calls=%fused_computation.75 | convolution fusion | flops 2408451 | bytes 1261568 | tf_op jit(solution)/shard_map/sub | solution.py:38
  180.0 0.0 copy-done.6
  180.0 2.9 %fusion.17 = bf16[4,128,8,72]{3,0,2,1:T(4,128)(2,1)S(1)} fusion(bf16[4,128,8,72]{3,0,2,1:T(4,128)(2,1)S(1)} %copy-done.6, f32[128,8,4,4]{2,3,1,0:T(4,128)} %get-tuple-element.24, f32[128,8,4]{2,1,0:T(8,128)} %get-tuple-element.23), kind=kOutput, calls=%fused_computation.35 | convolution fusion | flops 2686976 | bytes 1261568 | tf_op jit(solution)/shard_map/mhfg,gmhe->fmhe/dot_general | solution.py:67
  183.0 0.0 copy-start.9
  183.0 0.1 copy.27
  183.1 0.8 convert_element_type.72
  184.0 21.3 %all_to_all.11 = bf16[16,32,576]{2,1,0:T(8,128)(2,1)S(1)} all-to-all(bf16[16,32,576]{2,1,0:T(8,128)(2,1)S(1)} %convert_element_type.72), channel_id=1, replica_groups=mesh['groups'=2,'patch'=16] {'patch'}, dimensions={0} | all-to-all | bytes 1179648 | tf_op jit(solution)/shard_map/all_to_all | solution.py:143
  205.3 0.0 copy-done.9
  205.3 4.7 %fusion.7 = f32[512,1152]{1,0:T(8,128)} fusion(f32[512,1152]{1,0:T(8,128)} %copy-done.1, bf16[512,576]{1,0:T(8,128)(2,1)S(1)} %bitcast.62, bf16[576,1152]{1,0:T(8,128)(2,1)} %param.19, f32[1152]{0:T(1024)S(1)} %copy-done.9), kind=kOutput, calls=%fused_computation.14 | convolution fusion | flops 680656896 | bytes 6640128 | tf_op jit(solution)/shard_map/dot_general | solution.py:151
  (10 shorter events, 0.1 us)
Async XLA Ops:
  0.0 122.8 %copy-start = (bf16[576,1152]{1,0:T(8,128)(2,1)S(1)}, bf16[576,1152]{1,0:T(8,128)(2,1)}, u32[]{:S(2)}) copy-start(bf16[576,1152]{1,0:T(8,128)(2,1)} %param.17) | copy-start | bytes 3981316
  0.0 3.6 %collective-permute-start = (bf16[512,1152]{1,0:T(8,128)(2,1)}, bf16[512,1152]{1,0:T(8,128)(2,1)S(1)}, u32[]{:S(2)}, u32[]{:S(2)}) collective-permute-start(bf16[512,1152]{1,0:T(8,128)(2,1)} %param.11), channel_id=1, source_target_pairs={{0,1},{1,0},{2,3},{3,2},{4,5},{5,4},{6,7},{7,6},{8,9},{9,8},{10,11... | collective-permute-start | bytes 3538952 | tf_op jit(solution)/shard_map/ppermute | solution.py:17
  3.6 3.9 %copy-start.3 = (bf16[512,1152]{1,0:T(8,128)(2,1)}, bf16[512,1152]{1,0:T(8,128)(2,1)S(1)}, u32[]{:S(2)}) copy-start(bf16[512,1152]{1,0:T(8,128)(2,1)S(1)} %collective-permute-done) | copy-start | bytes 3538948
  7.5 54.7 %collective-permute-start.1 = (bf16[2,512,1152]{2,1,0:T(8,128)(2,1)}, bf16[2,512,1152]{2,1,0:T(8,128)(2,1)}, u32[]{:S(2)}, u32[]{:S(2)}) collective-permute-start(bf16[2,512,1152]{2,1,0:T(8,128)(2,1)} %maximum_select_fusion.2), channel_id=1, source_target_pairs={{0,2},{1,3},{2,0},{3,1},{4,6},{5,7},{6,4},{7,5},{8,10},{9,11},{10,... | collective-permute-start | bytes 7077896 | tf_op jit(solution)/shard_map/ppermute | solution.py:17
  17.6 4.8 %copy-start.11 = (s32[4]{0:T(128)S(1)}, s32[4]{0:T(128)}, u32[]{:S(2)}) copy-start(s32[4]{0:T(128)} %param.15) | copy-start | bytes 52
  17.6 6.2 %copy-start.2 = (bf16[512,1152]{1,0:T(8,128)(2,1)S(1)}, bf16[512,1152]{1,0:T(8,128)(2,1)}, u32[]{:S(2)}) copy-start(bf16[512,1152]{1,0:T(8,128)(2,1)} %param.11) | copy-start | bytes 3538948
  62.2 3.1 %copy-start.5 = (bf16[512,576]{1,0:T(8,128)(2,1)S(1)}, bf16[512,576]{1,0:T(8,128)(2,1)}, u32[]{:S(2)}) copy-start(bf16[512,576]{1,0:T(8,128)(2,1)} %copy.19) | copy-start | bytes 1769476
  85.4 5.9 %copy-start.8 = (bf16[1,512,576]{1,2,0:T(8,128)(2,1)S(1)}, bf16[1,512,576]{1,2,0:T(8,128)(2,1)}, u32[]{:S(2)}) copy-start(bf16[1,512,576]{1,2,0:T(8,128)(2,1)} %get-tuple-element.17) | copy-start | bytes 1769476
  108.6 14.1 %copy-start.4 = (bf16[512,1152]{1,0:T(8,128)(2,1)S(1)}, bf16[512,1152]{1,0:T(8,128)(2,1)}, u32[]{:S(2)}) copy-start(bf16[512,1152]{1,0:T(8,128)(2,1)} %param.10) | copy-start | bytes 3538948
  124.2 1.4 copy-start.1
  124.6 36.6 %copy-start.10 = (bf16[3,1152,576]{1,2,0:T(8,128)(2,1)S(1)}, bf16[3,1152,576]{1,2,0:T(8,128)(2,1)}, u32[]{:S(2)}) copy-start(bf16[3,1152,576]{1,2,0:T(8,128)(2,1)} %param.18) | copy-start | bytes 11943940
  170.8 2.5 %copy-start.7 = (bf16[4,128,8,72]{3,0,2,1:T(4,128)(2,1)S(1)}, bf16[4,128,8,72]{3,0,2,1:T(4,128)(2,1)}, u32[]{:S(2)}) copy-start(bf16[4,128,8,72]{3,0,2,1:T(4,128)(2,1)} %copy.23) | copy-start | bytes 1769476
  173.3 6.7 %copy-start.6 = (bf16[4,128,8,72]{3,0,2,1:T(4,128)(2,1)S(1)}, bf16[4,128,8,72]{3,0,2,1:T(4,128)(2,1)}, u32[]{:S(2)}) copy-start(bf16[4,128,8,72]{3,0,2,1:T(4,128)(2,1)} %copy.25) | copy-start | bytes 1769476
  183.0 22.3 %copy-start.9 = (f32[1152]{0:T(1024)S(1)}, f32[1152]{0:T(1024)}, u32[]{:S(2)}) copy-start(f32[1152]{0:T(1024)} %get-tuple-element.5) | copy-start | bytes 13828
where the time goes:
time: 211 us; the launch traced here: 210 us
  blocking collectives  56.9 us (27%)
  matrix products  54.9 us (26%)
  local copies, waits for them, and re-layouts  38.4 us (18%)
  waiting for transfers between devices  36.3 us (17%)
  other arithmetic  18.9 us (9%)
  starting transfers between devices  3.11 us (1%)
    ppermute x2, waiting for transfers between devices, from_partner(): return lax.ppermute(value, axis, pairs)  36.3 us
    all_to_all x1, blocking collectives, per_device(): lax.all_to_all(temporal_in.reshape(devices, piece_rows, feature_width), '...  35.6 us
    sub x2, matrix products, softmax_rows(): exp_scores = jnp.exp(scores - row_top)  24 us
    all_to_all x1, blocking collectives, per_device(): lax.all_to_all(mixed_out.reshape(devices, piece_rows, width_win), 'patch'...  21.3 us
    dot_general x1, matrix products, spatial_attend(): jnp.einsum('hqk,khe->qhe', weights, value_heads, preferred_element_type=j...  14.1 us
    select_n x3, other arithmetic, per_device(): jnp.where(low_half, jnp.stack([kv_block, partner], 0), jnp.stack([partner...  8.99 us
    another operation x1, local copies, waits for them, and re-layouts, spatial_attend(): key_heads = key_rows.reshape(-1, head_count, head_dim)  5.92 us
    another operation x1, local copies, waits for them, and re-layouts, spatial_attend(): value_heads = value_rows.reshape(-1, head_count, head_dim)  5.85 us
  transfers between devices with their start and end apart: 2, of which 1 were waited for; matrix products, arithmetic and copies ran while one was open for 8% of the time, Pallas kernels for 0%

commit v1 on v0

v1 whole, which is shorter than its diff:
```python
import functools
import math

import jax
import jax.numpy as jnp
from jax import lax
from jax.experimental import pallas as pl
from jax.experimental.pallas import tpu as pltpu
from jax.sharding import PartitionSpec as P

HEADS = 16
LANES = 128

epsilon = 1e-06


def swap_bit(value, axis, distance):
    mask = 2**distance
    pairs = [(source, source ^ mask) for source in range(lax.axis_size(axis))]
    return lax.ppermute(value, axis, pairs)


def normalize(activations):
    row_mean = jnp.mean(activations, axis=-1, keepdims=True)
    centered = activations - row_mean
    variance = jnp.mean(centered * centered, axis=-1, keepdims=True)
    return centered * lax.rsqrt(variance + epsilon)


def sinusoid(position, feature_width):
    half_width = feature_width // 2
    frequencies = jnp.exp(
        -math.log(10000.0) * jnp.arange(half_width, dtype=jnp.float32) / half_width
    )
    angles = jnp.asarray(position).astype(jnp.float32)[..., None] * frequencies
    return jnp.concatenate([jnp.sin(angles), jnp.cos(angles)], axis=-1)


def up_to_lanes(count):
    return -(-count // LANES) * LANES


def window(first, count):
    start, stop = first // LANES * LANES, up_to_lanes(first + count)
    lane = lax.broadcasted_iota(jnp.int32, (1, stop - start), 1) + start
    return start, stop, (lane >= first) & (lane < first + count)


def head_scores(q_rows, kv_refs, head, head_dim):
    start, stop, own = window(head * head_dim, head_dim)
    q_head = jnp.where(own, q_rows[:, start:stop], jnp.zeros((), q_rows.dtype))
    return [
        lax.dot_general(
            q_head, kv[:, start:stop], (((1,), (1,)), ((), ())), preferred_element_type=jnp.float32
        )
        for kv in kv_refs
    ]


def row_max(scores):
    top = scores[0]
    for more in scores[1:]:
        top = jnp.maximum(top, more)
    return jnp.max(top, axis=-1, keepdims=True)


def weigh(scores, top, kv_refs, head, head_dim, width_win):
    factor = head_dim**-0.5 * math.log2(math.e)
    exps = [jnp.exp2((part - top) * factor) for part in scores]
    total = exps[0]
    for more in exps[1:]:
        total = total + more
    total = jnp.sum(total, axis=-1, keepdims=True)
    start, stop, own = window(width_win + head * head_dim, head_dim)
    mixed = None
    for part, kv in zip(exps, kv_refs):
        term = jnp.dot(
            part.astype(jnp.bfloat16), kv[:, start:stop], preferred_element_type=jnp.float32
        )
        mixed = term if mixed is None else mixed + term
    return total, jnp.where(own, mixed, 0.0), start, stop


def near_kernel(head_dim, width_win, q_ref, kv0_ref, kv1_ref, acc_ref, top_ref, sum_ref):
    base = width_win // LANES * LANES
    kv_refs = (kv0_ref, kv1_ref)
    q_rows = q_ref[...]
    acc_ref[...] = jnp.zeros_like(acc_ref)
    for head in range(width_win // head_dim):
        scores = head_scores(q_rows, kv_refs, head, head_dim)
        top = row_max(scores)
        total, mixed, start, stop = weigh(scores, top, kv_refs, head, head_dim, width_win)
        acc_ref[:, start - base : stop - base] += mixed
        top_ref[:, head : head + 1] = top
        sum_ref[:, head : head + 1] = total


def far_rows(head_dim, width_win, q_rows, kv_refs, acc, top_old, sum_old):
    base = width_win // LANES * LANES
    factor = head_dim**-0.5 * math.log2(math.e)
    tiles = [None] * ((2 * width_win - base) // LANES)
    for head in range(width_win // head_dim):
        scores = head_scores(q_rows, kv_refs, head, head_dim)
        before = top_old[:, head : head + 1]
        top = jnp.maximum(row_max(scores), before)
        total, mixed, start, stop = weigh(scores, top, kv_refs, head, head_dim, width_win)
        shrink = jnp.exp2((before - top) * factor)
        inverse = 1.0 / (total + sum_old[:, head : head + 1] * shrink)
        _, _, own = window(width_win + head * head_dim, head_dim)
        earlier = acc[:, start - base : stop - base] * jnp.where(own, shrink, 0.0)
        share = (mixed + earlier) * inverse
        for tile in range((stop - start) // LANES):
            at = (start - base) // LANES + tile
            piece = share[:, tile * LANES : (tile + 1) * LANES]
            tiles[at] = piece if tiles[at] is None else tiles[at] + piece
    return jnp.concatenate(tiles, axis=1).astype(jnp.bfloat16)


def spatial_finish(mixed, tokens, out_weight, mod, position):
    projected = jnp.dot(mixed, out_weight, preferred_element_type=jnp.float32)
    after = tokens.astype(jnp.float32) + mod[2:3] * projected
    temporal_in = normalize(after) * (1.0 + mod[4:5]) + mod[3:4] + position
    return after, temporal_in.astype(jnp.bfloat16)


def far_kernel(
    head_dim, width_win, q_ref, kv2_ref, kv3_ref, acc_ref, top_ref, sum_ref, tokens_ref,
    out_weight_ref, mod_ref, after_ref, temporal_ref,
):
    mixed = far_rows(
        head_dim, width_win, q_ref[...], (kv2_ref, kv3_ref), acc_ref, top_ref, sum_ref
    )
    after, temporal_in = spatial_finish(
        mixed, tokens_ref[...], out_weight_ref[...], mod_ref[...], mod_ref[6:7]
    )
    after_ref[...] = after
    temporal_ref[...] = temporal_in


def temporal_rows(head_dim, rows, weight, frames):
    width_win = weight.shape[2]
    count = rows.shape[0]
    pixels = count // frames
    q, k, v = (
        jnp.dot(rows, weight[part], preferred_element_type=jnp.float32).astype(jnp.bfloat16)
        for part in range(3)
    )
    feature = lax.broadcasted_iota(jnp.int32, (width_win, LANES), 0)
    head = lax.broadcasted_iota(jnp.int32, (width_win, LANES), 1)
    gather = ((feature >= head * head_dim) & (feature < (head + 1) * head_dim)).astype(jnp.bfloat16)
    feature = lax.broadcasted_iota(jnp.int32, (LANES, width_win), 1)
    head = lax.broadcasted_iota(jnp.int32, (LANES, width_win), 0)
    spread = ((feature >= head * head_dim) & (feature < (head + 1) * head_dim)).astype(jnp.bfloat16)
    k_wide, v_wide = k.astype(jnp.float32), v.astype(jnp.float32)
    outs = []
    for frame in range(frames):
        q_frame = q[frame * pixels : (frame + 1) * pixels].astype(jnp.float32)
        products = jnp.concatenate(
            [q_frame * k_wide[g * pixels : (g + 1) * pixels] for g in range(frames)], axis=0
        )
        high = products.astype(jnp.bfloat16)
        low = (products - high.astype(jnp.float32)).astype(jnp.bfloat16)
        scores = jnp.dot(high, gather, preferred_element_type=jnp.float32) + jnp.dot(
            low, gather, preferred_element_type=jnp.float32
        )
        scores = [scores[g * pixels : (g + 1) * pixels] * head_dim**-0.5 for g in range(frames)]
        top = functools.reduce(jnp.maximum, scores)
        exps = [jnp.exp(part - top) for part in scores]
        inverse = 1.0 / functools.reduce(jnp.add, exps)
        weights = jnp.concatenate([part * inverse for part in exps], axis=0).astype(jnp.bfloat16)
        spread_weights = jnp.dot(weights, spread, preferred_element_type=jnp.float32)
        terms = spread_weights * v_wide
        mixed = functools.reduce(
            jnp.add, [terms[g * pixels : (g + 1) * pixels] for g in range(frames)]
        )
        outs.append(mixed.astype(jnp.bfloat16))
    return outs


def temporal_kernel(head_dim, frames, rows_ref, weight_ref, out_ref):
    outs = temporal_rows(head_dim, rows_ref[...], weight_ref, frames)
    pixels = rows_ref.shape[0] // frames
    for frame in range(frames):
        out_ref[frame * pixels : (frame + 1) * pixels] = outs[frame]


def cost(flops, nbytes, exps=0):
    return pl.CostEstimate(flops=int(flops), bytes_accessed=int(nbytes), transcendentals=int(exps))


def per_device(
    tokens,
    stale_kv,
    mod_table,
    mod_mix,
    timestep,
    frame_order,
    spatial_qkv,
    spatial_out,
    temporal_qkv,
    temporal_out,
):
    devices = lax.axis_size("patch")
    dev_index = lax.axis_index("patch")
    frames = devices // 4
    frame_slot = dev_index // 4
    row_count, feature_width = tokens.shape
    width_win = spatial_out.shape[0]
    head_dim = feature_width // HEADS
    base = width_win // LANES * LANES
    q_width = up_to_lanes(width_win)
    v_width = 2 * width_win - base

    kv2 = swap_bit(stale_kv, "patch", 1)
    kv1 = swap_bit(stale_kv, "patch", 0)
    modulation = mod_table + mod_mix * sinusoid(timestep[0], feature_width)[None, :]
    frame_id = jnp.sum(jnp.where(jnp.arange(frames) == frame_slot, frame_order, 0))
    position = sinusoid(frame_id, feature_width)[None, :]
    mod = jnp.concatenate([modulation, position, jnp.zeros_like(position)], axis=0)
    tokens_wide = tokens.astype(jnp.float32)
    spatial_in = (normalize(tokens_wide) * (1.0 + modulation[1]) + modulation[0]).astype(
        jnp.bfloat16
    )
    fresh = jnp.einsum(
        "tr,jrd->jtd", spatial_in, spatial_qkv, preferred_element_type=jnp.float32
    ).astype(jnp.bfloat16)
    q = jnp.pad(fresh[0], ((0, 0), (0, q_width - width_win)))
    kv0 = jnp.concatenate([fresh[1], fresh[2]], axis=1)
    out_weight = jnp.pad(spatial_out, ((width_win - base, 0), (0, 0)))

    block = min(128, row_count)
    steps = row_count // block
    whole = lambda a: pl.BlockSpec(a.shape, lambda i: (0,) * a.ndim)
    rows_of = lambda width: pl.BlockSpec((block, width), lambda i: (i, 0))
    half_flops = 4 * row_count * (2 * row_count) * width_win
    acc, top, total = pl.pallas_call(
        functools.partial(near_kernel, head_dim, width_win),
        grid=(steps,),
        in_specs=[rows_of(q_width), whole(kv0), whole(kv1)],
        out_specs=[rows_of(v_width), rows_of(LANES), rows_of(LANES)],
        out_shape=[
            jax.ShapeDtypeStruct((row_count, v_width), jnp.float32),
            jax.ShapeDtypeStruct((row_count, LANES), jnp.float32),
            jax.ShapeDtypeStruct((row_count, LANES), jnp.float32),
        ],
        cost_estimate=cost(4 * half_flops, 6e6),
        name="near_attention",
    )(q, kv0, kv1)
    kv3 = swap_bit(kv2, "patch", 0)
    after_spatial, temporal_in = pl.pallas_call(
        functools.partial(far_kernel, head_dim, width_win),
        grid=(steps,),
        in_specs=[
            rows_of(q_width), whole(kv2), whole(kv3), rows_of(v_width), rows_of(LANES),
            rows_of(LANES), rows_of(feature_width), whole(out_weight), whole(mod),
        ],
        out_specs=[rows_of(feature_width), rows_of(feature_width)],
        out_shape=[
            jax.ShapeDtypeStruct((row_count, feature_width), jnp.float32),
            jax.ShapeDtypeStruct((row_count, feature_width), jnp.bfloat16),
        ],
        cost_estimate=cost(4 * half_flops, 1e7),
        name="far_attention",
    )(q, kv2, kv3, acc, top, total, tokens, out_weight, mod)

    pixels = row_count // frames
    groups = [[4 * f + c for f in range(frames)] for c in range(4)]
    exchange = functools.partial(
        lax.all_to_all, axis_name="patch", split_axis=0, concat_axis=0,
        axis_index_groups=groups, tiled=True,
    )
    arranged = exchange(temporal_in)
    mixed = pl.pallas_call(
        functools.partial(temporal_kernel, head_dim, frames),
        in_specs=[pl.BlockSpec(memory_space=pltpu.VMEM)] * 2,
        out_specs=pl.BlockSpec(memory_space=pltpu.VMEM),
        out_shape=jax.ShapeDtypeStruct((row_count, width_win), jnp.bfloat16),
        cost_estimate=cost(6 * row_count * feature_width * width_win, 6e6),
        compiler_params=pltpu.CompilerParams(vmem_limit_bytes=60 * 1024 * 1024),
        name="temporal_attention",
    )(arranged, temporal_qkv)
    temporal_mixed = exchange(mixed)
    projected = jnp.dot(temporal_mixed, temporal_out, preferred_element_type=jnp.float32)
    return after_spatial + modulation[5] * projected


def solution(mesh):
    return jax.shard_map(
        per_device,
        mesh=mesh,
        in_specs=(
            P(("groups", "patch"), None),
            P(("groups", "patch"), None),
            P(),
            P(),
            P("groups"),
            P("groups"),
            P(),
            P(),
            P(),
            P(),
        ),
        out_specs=P(("groups", "patch"), None),
        check_vma=False,
    )
```

time: 211 us -> 139 us (0.66)
  matrix products: 54.9 us -> 7.22 us
  Pallas kernels: 0 us -> 46.8 us
  blocking collectives: 56.9 us -> 18.1 us
  local copies, waits for them, and re-layouts: 38.4 us -> 17 us
  other arithmetic: 18.9 us -> 7.87 us
  starting transfers between devices: 3.11 us -> 8.25 us
  waiting for transfers between devices: 36.3 us -> 31.5 us
    pallas_call x0 -> x3, Pallas kernels: none -> 46.8 us  [the longest x1 22.2 us: per_device(): pl.pallas_call(functools.partial(far_kernel, head_dim, width_win), grid=(...]
    all_to_all x2 -> x1, blocking collectives: 56.9 us -> 18.1 us  [per_device(): temporal_mixed = exchange(mixed)]
    ppermute x2 -> x3, waiting for transfers between devices: 36.3 us -> 8.81 us  [swap_bit(): return lax.ppermute(value, axis, pairs)]
    sub x2 -> x0, matrix products: 24 us -> none  [softmax_rows(): exp_scores = jnp.exp(scores - row_top)]
    all_to_all x0 -> x1, waiting for transfers between devices: none -> 22.7 us  [per_device(): arranged = exchange(temporal_in)]
    another operation x8 -> x0, local copies, waits for them, and re-layouts: 21.1 us -> none  [the longest x1 5.92 us: spatial_attend(): key_heads = key_rows.reshape(-1, head_count, head_dim)]
    dot_general x4 -> x0, matrix products: 21 us -> none  [the longest x1 14.1 us: spatial_attend(): jnp.einsum('hqk,khe->qhe', weights, value_heads, preferred_element_type=j...]
    select_n x4 -> x0, other arithmetic: 12.4 us -> none  [the longest x3 8.99 us: per_device(): jnp.where(low_half, jnp.stack([kv_block, partner], 0), jnp.stack([partner...]
  transfers between devices with their start and end apart: 2 -> 4, of which waited for: 1 -> 2; matrix products, arithmetic and copies ran while one was open for 8% -> 18% of each run, Pallas kernels for 0% -> 11%
where the time goes in v1:
time: 139 us; the launch traced here: 138 us
  Pallas kernels  46.8 us (34%)
  waiting for transfers between devices  31.5 us (23%)
  blocking collectives  18.1 us (13%)
  local copies, waits for them, and re-layouts  17 us (12%)
  starting transfers between devices  8.25 us (6%)
  other arithmetic  7.87 us (6%)
  matrix products  7.22 us (5%)
  between operations  1.44 us (1%)
    all_to_all x1, waiting for transfers between devices, per_device(): arranged = exchange(temporal_in)  22.7 us
    pallas_call x1, Pallas kernels, per_device(): pl.pallas_call(functools.partial(far_kernel, head_dim, width_win), grid=(...  22.2 us
    all_to_all x1, blocking collectives, per_device(): temporal_mixed = exchange(mixed)  18.1 us
    pallas_call x1, Pallas kernels, per_device(): pl.pallas_call(functools.partial(near_kernel, head_dim, width_win), grid=...  15.1 us
    pallas_call x1, Pallas kernels, per_device(): pl.pallas_call(functools.partial(temporal_kernel, head_dim, frames), in_s...  9.51 us
    unnamed x17, local copies, waits for them, and re-layouts  9.08 us
    ppermute x3, waiting for transfers between devices, swap_bit(): return lax.ppermute(value, axis, pairs)  8.81 us
    dot_general x1, matrix products, per_device(): jnp.einsum('tr,jrd->jtd', spatial_in, spatial_qkv, preferred_element_type...  6.03 us
  transfers between devices with their start and end apart: 4, of which 2 were waited for; matrix products, arithmetic and copies ran while one was open for 18% of the time, Pallas kernels for 11%

profile of v1, /device:TPU:0, one launch (start us, length us, event | category | flops | bytes accessed | tf_op | source)
XLA Modules:
  0.0 138.1 jit_solution(14882572423281692692)
XLA Ops:
  0.0 0.0 copy-start
  0.0 0.0 copy-start.1
  0.0 0.0 copy-start.5
  0.0 0.0 copy-start.4
  0.0 0.0 copy-start.7
  0.0 0.6 collective-permute-start.2
  0.6 2.6 %collective-permute-start = (bf16[512,1152]{1,0:T(8,128)(2,1)}, bf16[512,1152]{1,0:T(8,128)(2,1)}, u32[]{:S(2)}, u32[]{:S(2)}) collective-permute-start(bf16[512,1152]{1,0:T(8,128)(2,1)} %param.11), channel_id=1, source_target_pairs={{0,2},{1,3},{2,0},{3,1},{4,6},{5,7},{6,4},{7,5},{8,10},{9,11},{10,... | collective-permute-start | bytes 3538952 | tf_op jit(solution)/shard_map/ppermute | solution.py:20
  3.8 1.5 %convert_reduce_fusion = f32[512]{0:T(512)S(1)} fusion(bf16[512,1152]{1,0:T(8,128)(2,1)} %tokens_ref.1), kind=kLoop, calls=%fused_computation.2 | loop fusion | flops 1179136 | bytes 1181696 | tf_op jit(solution)/shard_map/reduce_sum | solution.py:24
  5.3 1.7 %fusion.2 = f32[512]{0:T(512)S(1)} fusion(bf16[512,1152]{1,0:T(8,128)(2,1)} %tokens_ref.1, f32[512]{0:T(512)S(1)} %broadcast_multiply_fusion), kind=kLoop, calls=%fused_computation.5 | loop fusion | flops 2358784 | bytes 1183744 | tf_op jit(solution)/shard_map/reduce_sum | solution.py:26
  7.1 0.1 fusion.17
  7.1 0.1 pad_maximum_fusion.1
  7.2 0.0 copy-done.5
  7.2 0.0 copy-done.4
  7.3 0.0 copy-done.7
  7.3 0.6 fusion.21
  8.6 0.0 copy-done.1
  8.6 6.0 %convolution_convert_fusion = bf16[512,3,576]{0,2,1:T(8,128)(2,1)} fusion(bf16[3,1152,576]{1,2,0:T(8,128)(2,1)} %param.16, bf16[512,1152]{1,0:T(8,128)(2,1)S(1)} %copy-done.1, f32[1152]{0:T(1024)S(1)} %get-tuple-element.16, f32[1152]{0:T(1024)S(1)} %get-tuple-element.17, f32[512]{0:T(512)S(1)} %add_rsqrt_fusion, f32[512]{0:T(512)S(1)} %broadcast_multiply_fusion), kind=kOutput, calls=%fused_computation.9 | convolution fusion | flops 2042855424 | bytes 6943744 | tf_op jit(solution)/shard_map/tr,jrd->jtd/dot_general | solution.py:224
  14.7 0.1 pad_maximum_fusion.2
  14.8 2.7 %copy.20 = bf16[512,3,576]{2,0,1:T(8,128)(2,1)S(1)} copy(bf16[512,3,576]{0,2,1:T(8,128)(2,1)} %convolution_convert_fusion) | data formatting | bytes 3538944 | tf_op jit(solution)/shard_map/convert_element_type | solution.py:226
  17.5 2.6 %pad.9.out_weight_ref = bf16[640,1152]{1,0:T(8,128)(2,1)} pad(bf16[576,1152]{1,0:T(8,128)(2,1)} %param.17, bf16[]{:T(256)} %constant.32.clone.1), padding=64_0x0_0 | pad | bytes 2801666 | tf_op jit(solution)/shard_map/jit(_pad)/pad | solution.py:229
  20.1 0.2 slice_bitcast_fusion.1
  20.3 0.9 pad.8.q_ref
  21.2 0.1 pad.12.clone
  21.2 8.8 %collective-permute-done.kv2_ref = bf16[512,1152]{1,0:T(8,128)(2,1)} collective-permute-done((bf16[512,1152]{1,0:T(8,128)(2,1)}, bf16[512,1152]{1,0:T(8,128)(2,1)}, u32[]{:S(2)}, u32[]{:S(2)}) %collective-permute-start) | collective-permute-done | bytes 1179680 | tf_op jit(solution)/shard_map/ppermute | solution.py:20
  30.0 0.0 collective-permute-start.1
  30.1 1.4 pad_maximum_fusion.kv0_ref
  31.4 0.7 maximum_maximum_fusion.mod_ref
  32.1 0.0 collective-permute-done.2.kv1_ref
  32.1 15.1 %near_attention.1 = (f32[512,640]{1,0:T(8,128)}, f32[512,128]{1,0:T(8,128)}, f32[512,128]{1,0:T(8,128)}) custom-call(bf16[512,640]{1,0:T(8,128)(2,1)} %pad.8.q_ref, bf16[512,1152]{1,0:T(8,128)(2,1)} %pad_maximum_fusion.kv0_ref, bf16[512,1152]{1,0:T(8,128)(2,1)} %collective-permute-done.2.kv1_ref), custom_call_target="tpu_custom_call" | custom-call | flops 4831838208 | bytes 6000000 | tf_op jit(solution)/shard_map/near_attention/pallas_call | solution.py:236
  47.2 0.0 collective-permute-done.1.kv3_ref
  47.2 0.0 copy-start.6
  47.2 1.0 copy-done.6
  48.3 22.2 %far_attention.1 = (f32[512,1152]{1,0:T(8,128)}, bf16[512,1152]{1,0:T(8,128)(2,1)}) custom-call(bf16[512,640]{1,0:T(8,128)(2,1)} %pad.8.q_ref, bf16[512,1152]{1,0:T(8,128)(2,1)} %collective-permute-done.kv2_ref, bf16[512,1152]{1,0:T(8,128)(2,1)} %copy-done.6, f32[512,640]{1,0:T(8,128)} %get-tuple-element.10.acc_ref, f32[512,128]{1,0:T(8,128)} %get-tuple-element.11.top_ref, ...), custom_call_target="tpu_custom_call" | custom-call | flops 4831838208 | bytes 10000000 | tf_op jit(solution)/shard_map/far_attention/pallas_call | solution.py:250
  70.5 5.1 %all-to-all-start = ((bf16[4,128,1152]{2,1,0:T(8,128)(2,1)}), bf16[4,128,1152]{2,1,0:T(8,128)(2,1)S(1)}, u32[]{:S(2)}, u32[]{:S(2)}) async-start(bf16[4,128,1152]{2,1,0:T(8,128)(2,1)} %bitcast.25), calls=%async_computation | async-start | bytes 2359296 | tf_op jit(solution)/shard_map/all_to_all | solution.py:272
  75.6 6.5 %copy.21.weight_ref = bf16[3,1152,576]{2,1,0:T(8,128)(2,1)} copy(bf16[3,1152,576]{1,2,0:T(8,128)(2,1)} %param.18) | data formatting | bytes 7962624 | tf_op args[8]
  82.1 22.7 %all-to-all-done = bf16[4,128,1152]{2,1,0:T(8,128)(2,1)S(1)} async-done(((bf16[4,128,1152]{2,1,0:T(8,128)(2,1)}), bf16[4,128,1152]{2,1,0:T(8,128)(2,1)S(1)}, u32[]{:S(2)}, u32[]{:S(2)}) %all-to-all-start) | async-done | bytes 1179680 | tf_op jit(solution)/shard_map/all_to_all | solution.py:272
  104.8 0.0 copy-start.3
  104.8 1.0 copy-done.3
  105.8 9.5 %temporal_attention.1 = bf16[512,576]{1,0:T(8,128)(2,1)} custom-call(bf16[512,1152]{1,0:T(8,128)(2,1)} %bitcast.26, bf16[3,1152,576]{2,1,0:T(8,128)(2,1)} %copy.21.weight_ref), custom_call_target="tpu_custom_call" | custom-call | flops 2038431744 | bytes 6000000 | tf_op jit(solution)/shard_map/temporal_attention/pallas_call | solution.py:273
  115.3 1.4 %copy.22 = bf16[4,128,576]{1,2,0:T(8,128)(2,1)S(1)} copy(bf16[4,128,576]{2,1,0:T(8,128)(2,1)} %bitcast.27) | data formatting | bytes 1179648 | tf_op jit(solution)/shard_map/all_to_all | solution.py:282
  116.7 18.1 %all_to_all.23 = bf16[4,128,576]{1,2,0:T(8,128)(2,1)S(1)} all-to-all(bf16[4,128,576]{1,2,0:T(8,128)(2,1)S(1)} %copy.22), channel_id=1, replica_groups={{0,4,8,12},{1,5,9,13},{2,6,10,14},{3,7,11,15},{16,20,24,28},{17,21,25,2..., dimensions={0} | all-to-all | bytes 1179648 | tf_op jit(solution)/shard_map/all_to_all | solution.py:282
  134.8 0.0 copy-done
  134.8 0.0 copy-start.2
  134.8 1.2 convolution_multiply_fusion
  136.0 0.5 copy-done.2
  136.5 1.6 %add.47 = f32[512,1152]{1,0:T(8,128)} add(f32[512,1152]{1,0:T(8,128)S(1)} %copy-done.2, f32[512,1152]{1,0:T(8,128)S(1)} %convolution_multiply_fusion) | non-fusion elementwise | flops 589824 | bytes 7077888 | tf_op jit(solution)/shard_map/add | solution.py:284
  (6 shorter events, 0.1 us)
Async XLA Ops:
  0.0 134.8 %copy-start = (bf16[576,1152]{1,0:T(8,128)(2,1)S(1)}, bf16[576,1152]{1,0:T(8,128)(2,1)}, u32[]{:S(2)}) copy-start(bf16[576,1152]{1,0:T(8,128)(2,1)} %param.19) | copy-start | bytes 3981316
  0.0 8.6 %copy-start.1 = (bf16[512,1152]{1,0:T(8,128)(2,1)S(1)}, bf16[512,1152]{1,0:T(8,128)(2,1)}, u32[]{:S(2)}) copy-start(bf16[512,1152]{1,0:T(8,128)(2,1)} %tokens_ref.1) | copy-start | bytes 3538948
  0.0 7.2 %copy-start.5 = (f32[6,1152]{1,0:T(8,128)S(1)}, f32[6,1152]{1,0:T(8,128)}, u32[]{:S(2)}) copy-start(f32[6,1152]{1,0:T(8,128)} %param.13) | copy-start | bytes 82948
  0.0 7.2 %copy-start.4 = (f32[6,1152]{1,0:T(8,128)S(1)}, f32[6,1152]{1,0:T(8,128)}, u32[]{:S(2)}) copy-start(f32[6,1152]{1,0:T(8,128)} %param.12) | copy-start | bytes 82948
  0.0 7.3 %copy-start.7 = (s32[4]{0:T(128)S(1)}, s32[4]{0:T(128)}, u32[]{:S(2)}) copy-start(s32[4]{0:T(128)} %param.15) | copy-start | bytes 52
  0.0 32.1 %collective-permute-start.2 = (bf16[512,1152]{1,0:T(8,128)(2,1)}, bf16[512,1152]{1,0:T(8,128)(2,1)}, u32[]{:S(2)}, u32[]{:S(2)}) collective-permute-start(bf16[512,1152]{1,0:T(8,128)(2,1)} %param.11), channel_id=1, source_target_pairs={{0,1},{1,0},{2,3},{3,2},{4,5},{5,4},{6,7},{7,6},{8,9},{9,8},{10,11... | collective-permute-start | bytes 3538952 | tf_op jit(solution)/shard_map/ppermute | solution.py:20
  0.6 29.5 %collective-permute-start = (bf16[512,1152]{1,0:T(8,128)(2,1)}, bf16[512,1152]{1,0:T(8,128)(2,1)}, u32[]{:S(2)}, u32[]{:S(2)}) collective-permute-start(bf16[512,1152]{1,0:T(8,128)(2,1)} %param.11), channel_id=1, source_target_pairs={{0,2},{1,3},{2,0},{3,1},{4,6},{5,7},{6,4},{7,5},{8,10},{9,11},{10,... | collective-permute-start | bytes 3538952 | tf_op jit(solution)/shard_map/ppermute | solution.py:20
  30.0 17.2 %collective-permute-start.1 = (bf16[512,1152]{1,0:T(8,128)(2,1)}, bf16[512,1152]{1,0:T(8,128)(2,1)S(1)}, u32[]{:S(2)}, u32[]{:S(2)}) collective-permute-start(bf16[512,1152]{1,0:T(8,128)(2,1)} %collective-permute-done.kv2_ref), channel_id=1, source_target_pairs={{0,1},{1,0},{2,3},{3,2},{4,5},{5,4},{6,7},{7,6},{8,9},{9,8},{10,11... | collective-permute-start | bytes 3538952 | tf_op jit(solution)/shard_map/ppermute | solution.py:20
  47.2 1.0 copy-start.6
  70.5 34.3 %all-to-all-start = ((bf16[4,128,1152]{2,1,0:T(8,128)(2,1)}), bf16[4,128,1152]{2,1,0:T(8,128)(2,1)S(1)}, u32[]{:S(2)}, u32[]{:S(2)}) async-start(bf16[4,128,1152]{2,1,0:T(8,128)(2,1)} %bitcast.25), calls=%async_computation | async-start | bytes 2359296 | tf_op jit(solution)/shard_map/all_to_all | solution.py:272
  104.8 1.0 copy-start.3
  134.8 1.7 %copy-start.2 = (f32[512,1152]{1,0:T(8,128)S(1)}, f32[512,1152]{1,0:T(8,128)}, u32[]{:S(2)}) copy-start(f32[512,1152]{1,0:T(8,128)} %get-tuple-element.13) | copy-start | bytes 7077892

commit v2 on v1

v2 whole, which is shorter than its diff:
```python
import functools
import math

import jax
import jax.numpy as jnp
from jax import lax
from jax.experimental import pallas as pl
from jax.experimental.pallas import tpu as pltpu
from jax.sharding import PartitionSpec as P

HEADS = 16
LANES = 128

epsilon = 1e-06


def normalize(activations):
    row_mean = jnp.mean(activations, axis=-1, keepdims=True)
    centered = activations - row_mean
    variance = jnp.mean(centered * centered, axis=-1, keepdims=True)
    return centered * lax.rsqrt(variance + epsilon)


def sinusoid(position, feature_width):
    half_width = feature_width // 2
    frequencies = jnp.exp(
        -math.log(10000.0) * jnp.arange(half_width, dtype=jnp.float32) / half_width
    )
    angles = jnp.asarray(position).astype(jnp.float32)[..., None] * frequencies
    return jnp.concatenate([jnp.sin(angles), jnp.cos(angles)], axis=-1)


def up_to_lanes(count):
    return -(-count // LANES) * LANES


def window(first, count):
    start, stop = first // LANES * LANES, up_to_lanes(first + count)
    lane = lax.broadcasted_iota(jnp.int32, (1, stop - start), 1) + start
    return start, stop, (lane >= first) & (lane < first + count)


def head_scores(q_rows, kv_refs, head, head_dim):
    start, stop, own = window(head * head_dim, head_dim)
    q_head = jnp.where(own, q_rows[:, start:stop], jnp.zeros((), q_rows.dtype))
    return [
        lax.dot_general(
            q_head, kv[:, start:stop], (((1,), (1,)), ((), ())), preferred_element_type=jnp.float32
        )
        for kv in kv_refs
    ]


def row_max(scores):
    top = scores[0]
    for more in scores[1:]:
        top = jnp.maximum(top, more)
    return jnp.max(top, axis=-1, keepdims=True)


def weigh(scores, top, kv_refs, head, head_dim, width_win):
    factor = head_dim**-0.5 * math.log2(math.e)
    exps = [jnp.exp2((part - top) * factor) for part in scores]
    total = exps[0]
    for more in exps[1:]:
        total = total + more
    total = jnp.sum(total, axis=-1, keepdims=True)
    start, stop, own = window(width_win + head * head_dim, head_dim)
    mixed = None
    for part, kv in zip(exps, kv_refs):
        term = jnp.dot(
            part.astype(jnp.bfloat16), kv[:, start:stop], preferred_element_type=jnp.float32
        )
        mixed = term if mixed is None else mixed + term
    return total, jnp.where(own, mixed, 0.0), start, stop


def near_rows(head_dim, width_win, q_rows, kv_refs, acc, top_ref, sum_ref, at, count):
    base = width_win // LANES * LANES
    heads = width_win // head_dim
    here = pl.ds(at, count)
    acc[here] = jnp.zeros((count,) + acc.shape[1:], acc.dtype)
    scores = head_scores(q_rows, kv_refs, 0, head_dim)
    for head in range(heads):
        later = head_scores(q_rows, kv_refs, head + 1, head_dim) if head + 1 < heads else None
        top = row_max(scores)
        total, mixed, start, stop = weigh(scores, top, kv_refs, head, head_dim, width_win)
        acc[here, :, start - base : stop - base] += mixed.reshape(count, -1, stop - start)
        top_ref[here, :, head : head + 1] = top.reshape(count, -1, 1)
        sum_ref[here, :, head : head + 1] = total.reshape(count, -1, 1)
        scores = later


def far_rows(head_dim, width_win, q_rows, kv_refs, acc, top_old, sum_old):
    base = width_win // LANES * LANES
    factor = head_dim**-0.5 * math.log2(math.e)
    tiles = [None] * ((2 * width_win - base) // LANES)
    heads = width_win // head_dim
    scores = head_scores(q_rows, kv_refs, 0, head_dim)
    for head in range(heads):
        later = head_scores(q_rows, kv_refs, head + 1, head_dim) if head + 1 < heads else None
        before = top_old[:, head : head + 1]
        top = jnp.maximum(row_max(scores), before)
        total, mixed, start, stop = weigh(scores, top, kv_refs, head, head_dim, width_win)
        shrink = jnp.exp2((before - top) * factor)
        inverse = 1.0 / (total + sum_old[:, head : head + 1] * shrink)
        _, _, own = window(width_win + head * head_dim, head_dim)
        earlier = acc[:, start - base : stop - base] * jnp.where(own, shrink, 0.0)
        share = (mixed + earlier) * inverse
        for tile in range((stop - start) // LANES):
            at = (start - base) // LANES + tile
            piece = share[:, tile * LANES : (tile + 1) * LANES]
            tiles[at] = piece if tiles[at] is None else tiles[at] + piece
        scores = later
    return jnp.concatenate(tiles, axis=1).astype(jnp.bfloat16)


def spatial_finish(mixed, tokens, out_weight, mod, position):
    projected = jnp.dot(mixed, out_weight, preferred_element_type=jnp.float32)
    after = tokens.astype(jnp.float32) + mod[2:3] * projected
    temporal_in = normalize(after) * (1.0 + mod[4:5]) + mod[3:4] + position
    return after, temporal_in.astype(jnp.bfloat16)


def times_transposed(rows, weight):
    return lax.dot_general(
        rows, weight, (((1,), (1,)), ((), ())), preferred_element_type=jnp.float32
    )


def temporal_rows(head_dim, rows, weight, frames):
    width_win = weight.shape[0] // 3
    count = rows.shape[0]
    pixels = count // frames
    q, k, v = (
        times_transposed(rows, weight[part * width_win : (part + 1) * width_win]).astype(jnp.bfloat16)
        for part in range(3)
    )
    feature = lax.broadcasted_iota(jnp.int32, (width_win, LANES), 0)
    head = lax.broadcasted_iota(jnp.int32, (width_win, LANES), 1)
    gather = ((feature >= head * head_dim) & (feature < (head + 1) * head_dim)).astype(jnp.bfloat16)
    feature = lax.broadcasted_iota(jnp.int32, (LANES, width_win), 1)
    head = lax.broadcasted_iota(jnp.int32, (LANES, width_win), 0)
    spread = ((feature >= head * head_dim) & (feature < (head + 1) * head_dim)).astype(jnp.bfloat16)
    k_wide, v_wide = k.astype(jnp.float32), v.astype(jnp.float32)
    outs = []
    for frame in range(frames):
        q_frame = q[frame * pixels : (frame + 1) * pixels].astype(jnp.float32)
        products = jnp.concatenate(
            [q_frame * k_wide[g * pixels : (g + 1) * pixels] for g in range(frames)], axis=0
        )
        high = products.astype(jnp.bfloat16)
        low = (products - high.astype(jnp.float32)).astype(jnp.bfloat16)
        scores = jnp.dot(high, gather, preferred_element_type=jnp.float32) + jnp.dot(
            low, gather, preferred_element_type=jnp.float32
        )
        scores = [scores[g * pixels : (g + 1) * pixels] * head_dim**-0.5 for g in range(frames)]
        top = functools.reduce(jnp.maximum, scores)
        exps = [jnp.exp(part - top) for part in scores]
        inverse = 1.0 / functools.reduce(jnp.add, exps)
        weights = jnp.concatenate([part * inverse for part in exps], axis=0).astype(jnp.bfloat16)
        spread_weights = jnp.dot(weights, spread, preferred_element_type=jnp.float32)
        terms = spread_weights * v_wide
        mixed = functools.reduce(
            jnp.add, [terms[g * pixels : (g + 1) * pixels] for g in range(frames)]
        )
        outs.append(mixed.astype(jnp.bfloat16))
    return outs


def block_kernel(
    head_dim, tokens_hbm, stale_hbm, spatial_w_hbm, spatial_o_hbm, temporal_w_hbm, temporal_o_hbm,
    mod_ref, out_ref, tokens, kv0, kv1, kv2, kv3, q, spatial_w, spatial_o, temporal_w, temporal_o,
    acc, top, total, leaving, arriving, mixed_out, mixed_in, load_sem, kv_send, kv_recv, in_send,
    in_recv, back_send, back_recv, own_sem,
):
    chunks, frames, pixels, _ = leaving.shape
    rows = frames * pixels
    width_win = temporal_o.shape[0]
    base = width_win // LANES * LANES
    device = lax.axis_index("patch")
    slot, quarter = device // 4, device % 4

    def flip(mask):
        bit = device // mask % 2
        return device + mask - 2 * mask * bit

    def peer(step):
        other = (slot + step) % frames
        return other, other * 4 + quarter

    loads = [
        pltpu.make_async_copy(source, target, load_sem.at[at])
        for at, (source, target) in enumerate(
            [
                (tokens_hbm, tokens),
                (spatial_w_hbm, spatial_w),
                (spatial_o_hbm, spatial_o.at[width_win - base :]),
                (temporal_w_hbm, temporal_w),
                (temporal_o_hbm, temporal_o),
            ]
        )
    ]
    for load in loads:
        load.start()

    barrier = pltpu.get_barrier_semaphore()
    others = [flip(2), flip(1)] + [peer(step)[1] for step in range(1, frames)]
    for other in others:
        pl.semaphore_signal(
            barrier, inc=1, device_id={"patch": other}, device_id_type=pl.DeviceIdType.MESH
        )
    pl.semaphore_wait(barrier, len(others))

    def remote(source, target, send, recv, other):
        return pltpu.make_async_remote_copy(
            src_ref=source, dst_ref=target, send_sem=send, recv_sem=recv,
            device_id={"patch": other}, device_id_type=pl.DeviceIdType.MESH,
        )

    across = remote(stale_hbm, kv2, kv_send.at[0], kv_recv.at[0], flip(2))
    beside = remote(stale_hbm, kv1, kv_send.at[1], kv_recv.at[1], flip(1))
    onward = remote(kv2, kv3, kv_send.at[2], kv_recv.at[2], flip(1))
    across.start()
    beside.start()

    spatial_o[: width_win - base] = jnp.zeros((width_win - base, spatial_o.shape[1]), jnp.bfloat16)
    loads[0].wait()
    loads[1].wait()

    def project(c, carry):
        wide = tokens[c].astype(jnp.float32)
        spatial_in = (normalize(wide) * (1.0 + mod_ref[1:2]) + mod_ref[0:1]).astype(jnp.bfloat16)
        here = pl.ds(pl.multiple_of(c * rows, rows), rows)
        fresh_q, fresh_k, fresh_v = (
            times_transposed(spatial_in, spatial_w[part * width_win : (part + 1) * width_win])
            .astype(jnp.bfloat16)
            for part in range(3)
        )
        q[c, :, :width_win] = fresh_q
        q[c, :, width_win:] = jnp.zeros((rows, q.shape[2] - width_win), jnp.bfloat16)
        kv0[here, :width_win] = fresh_k
        kv0[here, width_win:] = fresh_v
        return carry

    lax.fori_loop(0, chunks, project, 0)
    beside.wait_recv()

    near_count = 2 if chunks % 2 == 0 and rows <= 128 else 1

    def near(block, carry):
        at = block * near_count
        q_rows = q[pl.ds(at, near_count)].reshape(near_count * rows, q.shape[2])
        near_rows(head_dim, width_win, q_rows, (kv0, kv1), acc, top, total, at, near_count)
        return carry

    lax.fori_loop(0, chunks // near_count, near, 0)
    across.wait_recv()
    onward.start()
    loads[2].wait()
    loads[3].wait()
    loads[4].wait()
    onward.wait_recv()

    def inward(c, step):
        other, target = peer(step)
        return other, remote(
            leaving.at[c, other], arriving.at[c, slot], in_send.at[c, step], in_recv.at[c, step],
            target,
        )

    def backward(c, step):
        other, target = peer(step)
        return remote(
            mixed_out.at[c, other], mixed_in.at[c, slot], back_send.at[c, step],
            back_recv.at[c, step], target,
        )

    def keep(c):
        return pltpu.make_async_copy(leaving.at[c, slot], arriving.at[c, slot], own_sem.at[0, c])

    def keep_back(c):
        return pltpu.make_async_copy(mixed_out.at[c, slot], mixed_in.at[c, slot], own_sem.at[1, c])

    def far(c):
        mixed = far_rows(
            head_dim, width_win, q[c], (kv2, kv3), acc.at[c], top.at[c], total.at[c]
        )
        after, temporal_in = spatial_finish(
            mixed, tokens[c], spatial_o[...], mod_ref, mod_ref[6:7]
        )
        out_ref[c] = after
        leaving[c] = temporal_in.reshape(frames, pixels, temporal_in.shape[1])
        for step in range(1, frames):
            inward(c, step)[1].start()
        keep(c).start()

    def temporal(c):
        for step in range(1, frames):
            inward(c, step)[1].wait_recv()
        keep(c).wait()
        flat = arriving[c].reshape(rows, arriving.shape[3])
        for frame, mixed in enumerate(temporal_rows(head_dim, flat, temporal_w, frames)):
            mixed_out[c, frame] = mixed
        for step in range(1, frames):
            backward(c, step).start()
        keep_back(c).start()

    lag = min(2, chunks - 1)

    def first(c, carry):
        far(c)

        @pl.when(c >= lag)
        def _():
            temporal(c - lag)

        return carry

    def second(c, carry):
        temporal(c)
        return carry

    def third(c, carry):
        for step in range(1, frames):
            backward(c, step).wait_recv()
        keep_back(c).wait()
        mixed = mixed_in[c].reshape(rows, width_win)
        projected = jnp.dot(mixed, temporal_o[...], preferred_element_type=jnp.float32)
        out_ref[c] = out_ref[c] + mod_ref[5:6] * projected
        return carry

    lax.fori_loop(0, chunks, first, 0)
    lax.fori_loop(chunks - lag, chunks, second, 0)
    lax.fori_loop(0, chunks, third, 0)

    def drain(c, carry):
        for step in range(1, frames):
            inward(c, step)[1].wait_send()
            backward(c, step).wait_send()
        return carry

    lax.fori_loop(0, chunks, drain, 0)
    for copy in (across, beside, onward):
        copy.wait_send()


def per_device(
    tokens,
    stale_kv,
    mod_table,
    mod_mix,
    timestep,
    frame_order,
    spatial_qkv,
    spatial_out,
    temporal_qkv,
    temporal_out,
):
    devices = lax.axis_size("patch")
    dev_index = lax.axis_index("patch")
    frames = devices // 4
    frame_slot = dev_index // 4
    row_count, feature_width = tokens.shape
    width_win = spatial_out.shape[0]
    head_dim = feature_width // HEADS
    base = width_win // LANES * LANES
    q_width = up_to_lanes(width_win)
    v_width = 2 * width_win - base

    modulation = mod_table + mod_mix * sinusoid(timestep[0], feature_width)[None, :]
    frame_id = jnp.sum(jnp.where(jnp.arange(frames) == frame_slot, frame_order, 0))
    position = sinusoid(frame_id, feature_width)[None, :]
    mod = jnp.concatenate([modulation, position, jnp.zeros_like(position)], axis=0)
    chunks = max(1, min(4, row_count // (16 * frames)))
    rows = row_count // chunks
    pixels = rows // frames
    transposed = lambda w: jnp.swapaxes(w, 1, 2).reshape(3 * width_win, feature_width)
    flat = (row_count, feature_width)
    chunked = (chunks, rows, feature_width)
    exchanged = (chunks, frames, pixels)
    anywhere = pl.BlockSpec(memory_space=pl.ANY)
    bf16, f32 = jnp.bfloat16, jnp.float32
    out = pl.pallas_call(
        functools.partial(block_kernel, head_dim),
        in_specs=[anywhere] * 6 + [pl.BlockSpec(memory_space=pltpu.VMEM)],
        out_specs=pl.BlockSpec(memory_space=pltpu.VMEM),
        out_shape=jax.ShapeDtypeStruct(chunked, f32),
        scratch_shapes=[
            pltpu.VMEM(chunked, bf16),
            pltpu.VMEM(flat, bf16),
            pltpu.VMEM(flat, bf16),
            pltpu.VMEM(flat, bf16),
            pltpu.VMEM(flat, bf16),
            pltpu.VMEM((chunks, rows, q_width), bf16),
            pltpu.VMEM((3 * width_win, feature_width), bf16),
            pltpu.VMEM((v_width, feature_width), bf16),
            pltpu.VMEM((3 * width_win, feature_width), bf16),
            pltpu.VMEM((width_win, feature_width), bf16),
            pltpu.VMEM((chunks, rows, v_width), f32),
            pltpu.VMEM((chunks, rows, LANES), f32),
            pltpu.VMEM((chunks, rows, LANES), f32),
            pltpu.VMEM(exchanged + (feature_width,), bf16),
            pltpu.VMEM(exchanged + (feature_width,), bf16),
            pltpu.VMEM(exchanged + (width_win,), bf16),
            pltpu.VMEM(exchanged + (width_win,), bf16),
            pltpu.SemaphoreType.DMA((5,)),
            pltpu.SemaphoreType.DMA((3,)),
            pltpu.SemaphoreType.DMA((3,)),
            pltpu.SemaphoreType.DMA((chunks, frames)),
            pltpu.SemaphoreType.DMA((chunks, frames)),
            pltpu.SemaphoreType.DMA((chunks, frames)),
            pltpu.SemaphoreType.DMA((chunks, frames)),
            pltpu.SemaphoreType.DMA((2, chunks)),
        ],
        compiler_params=pltpu.CompilerParams(
            collective_id=0, has_side_effects=True, vmem_limit_bytes=60 * 1024 * 1024
        ),
        name="denoising_block",
    )(
        tokens.reshape(chunked), stale_kv, transposed(spatial_qkv), spatial_out,
        transposed(temporal_qkv), temporal_out, mod,
    )
    return out.reshape(flat)


def solution(mesh):
    return jax.shard_map(
        per_device,
        mesh=mesh,
        in_specs=(
            P(("groups", "patch"), None),
            P(("groups", "patch"), None),
            P(),
            P(),
            P("groups"),
            P("groups"),
            P(),
            P(),
            P(),
            P(),
        ),
        out_specs=P(("groups", "patch"), None),
        check_vma=False,
    )
```

time: 139 us -> 90.1 us (0.65)
  Pallas kernels: 46.8 us -> 81.6 us
  waiting for transfers between devices: 31.5 us -> 0 us
  blocking collectives: 18.1 us -> 0 us
  local copies, waits for them, and re-layouts: 17 us -> 3.3 us
  starting transfers between devices: 8.25 us -> 0 us
  matrix products: 7.22 us -> 0 us
  other arithmetic: 7.87 us -> 3.04 us
    pallas_call x3 -> x1, Pallas kernels: 46.8 us -> 81.6 us  [per_device(): pl.pallas_call(functools.partial(block_kernel, head_dim), in_specs=[anywh...]
    all_to_all x1 -> x0, waiting for transfers between devices: 22.7 us -> none  [per_device(): arranged = exchange(temporal_in)]
    all_to_all x1 -> x0, blocking collectives: 18.1 us -> none  [per_device(): temporal_mixed = exchange(mixed)]
    ppermute x3 -> x0, waiting for transfers between devices: 8.81 us -> none  [swap_bit(): return lax.ppermute(value, axis, pairs)]
    dot_general x2 -> x0, matrix products: 7.22 us -> none  [the longest x1 6.03 us: per_device(): jnp.einsum('tr,jrd->jtd', spatial_in, spatial_qkv, preferred_element_type...]
    unnamed x17 -> x1, local copies, waits for them, and re-layouts: 9.08 us -> 3.22 us
    all_to_all x1 -> x0, starting transfers between devices: 5.1 us -> none  [per_device(): arranged = exchange(temporal_in)]
    pad x2 -> x0, local copies, waits for them, and re-layouts: 3.48 us -> none  [the longest x1 2.57 us: per_device(): out_weight = jnp.pad(spatial_out, ((width_win - base, 0), (0, 0)))]
  transfers between devices with their start and end apart: 4 -> 0, of which waited for: 2 -> 0; matrix products, arithmetic and copies ran while one was open for 18% -> 0% of each run, Pallas kernels for 11% -> 0%
where the time goes in v2:
time: 90.1 us; the launch traced here: 89.2 us
  Pallas kernels  81.6 us (91%)
  local copies, waits for them, and re-layouts  3.3 us (4%)
  other arithmetic  3.04 us (3%)
  between operations  1.33 us (1%)
    pallas_call x1, Pallas kernels, per_device(): pl.pallas_call(functools.partial(block_kernel, head_dim), in_specs=[anywh...  81.6 us
    unnamed x1, local copies, waits for them, and re-layouts  3.22 us

profile of v2, /device:TPU:0, one launch (start us, length us, event | category | flops | bytes accessed | tf_op | source)
XLA Modules:
  0.0 89.2 jit_solution(9658936894450742579)
XLA Ops:
  0.7 1.3 %fusion.6 = s32[]{:T(128)} fusion(s32[4]{0:T(128)} %param.15, s32[]{:T(128)S(6)} %select_n.9), kind=kLoop, calls=%fused_computation.12 | loop fusion | flops 11 | bytes 24 | tf_op jit(solution)/shard_map/reduce_sum | solution.py:372
  2.6 0.1 pad.2.clone
  2.7 0.1 pad_maximum_fusion.1
  2.8 0.1 fusion.2
  2.9 0.1 pad_maximum_fusion
  2.9 0.8 multiply_add_fusion
  3.8 0.7 maximum_maximum_fusion.mod_ref
  4.4 81.6 %denoising_block.1 = f32[4,128,1152]{2,1,0:T(8,128)} custom-call(bf16[4,128,1152]{2,1,0:T(8,128)(2,1)} %bitcast.13, bf16[512,1152]{1,0:T(8,128)(2,1)} %stale_hbm.1, bf16[1728,1152]{1,0:T(8,128)(2,1)} %bitcast.11, bf16[576,1152]{1,0:T(8,128)(2,1)} %spatial_o_hbm.1, bf16[1728,1152]{1,0:T(8,128)(2,1)} %bitcast.12, bf16[576,1152]{1,0:T(8,128)(2,1)} %temporal_o_hbm.1, ...), custom_call_target="tpu_custom_call" | custom-call | tf_op jit(solution)/shard_map/denoising_block/pallas_call | solution.py:384
  86.0 3.2 %copy.13 = f32[512,1152]{1,0:T(8,128)} copy(f32[512,1152]{1,0:T(8,128)} %bitcast.10) | data formatting | bytes 4718592
  (2 shorter events, 0.1 us)

commit v3 on v2

--- a/solution.py
+++ b/solution.py
@@ -91,27 +91,60 @@
         scores = later
 
 
-def far_rows(head_dim, width_win, q_rows, kv_refs, acc, top_old, sum_old):
+def far_message(head_dim, width_win, q_rows, kv_refs):
     base = width_win // LANES * LANES
-    factor = head_dim**-0.5 * math.log2(math.e)
+    heads = width_win // head_dim
     tiles = [None] * ((2 * width_win - base) // LANES)
-    heads = width_win // head_dim
+    lane = lax.broadcasted_iota(jnp.int32, (1, LANES), 1)
+    stats = jnp.zeros((q_rows.shape[0], LANES), jnp.float32)
     scores = head_scores(q_rows, kv_refs, 0, head_dim)
     for head in range(heads):
         later = head_scores(q_rows, kv_refs, head + 1, head_dim) if head + 1 < heads else None
-        before = top_old[:, head : head + 1]
-        top = jnp.maximum(row_max(scores), before)
+        top = row_max(scores)
         total, mixed, start, stop = weigh(scores, top, kv_refs, head, head_dim, width_win)
-        shrink = jnp.exp2((before - top) * factor)
-        inverse = 1.0 / (total + sum_old[:, head : head + 1] * shrink)
-        _, _, own = window(width_win + head * head_dim, head_dim)
-        earlier = acc[:, start - base : stop - base] * jnp.where(own, shrink, 0.0)
-        share = (mixed + earlier) * inverse
+        own = lane % heads == head
+        stats = jnp.where(own & (lane < 3 * heads), top, stats)
+        stats = jnp.where(own & (lane >= 3 * heads) & (lane < 6 * heads), total, stats)
+        for tile in range((stop - start) // LANES):
+            at = (start - base) // LANES + tile
+            piece = mixed[:, tile * LANES : (tile + 1) * LANES]
+            tiles[at] = piece if tiles[at] is None else tiles[at] + piece
+        scores = later
+    high = stats.astype(jnp.bfloat16).astype(jnp.float32)
+    middle = (stats - high).astype(jnp.bfloat16).astype(jnp.float32)
+    low = stats - high - middle
+    part = lane // heads % 3
+    split = jnp.where(part == 0, high, jnp.where(part == 1, middle, low))
+    tiles[0] = jnp.where(lane < 6 * heads, split, tiles[0])
+    return jnp.concatenate(tiles, axis=1).astype(jnp.bfloat16)
+
+
+def join(head_dim, width_win, message, acc, top, total):
+    base = width_win // LANES * LANES
+    heads = width_win // head_dim
+    factor = head_dim**-0.5 * math.log2(math.e)
+    source = lax.broadcasted_iota(jnp.int32, (LANES, LANES), 0)
+    target = lax.broadcasted_iota(jnp.int32, (LANES, LANES), 1)
+    wanted = jnp.where(source < 3 * heads, source % heads, heads + source % heads)
+    picks = ((source < 6 * heads) & (target == wanted)).astype(jnp.bfloat16)
+    stats = jnp.dot(message[:, :LANES], picks, preferred_element_type=jnp.float32)
+    tiles = [None] * ((2 * width_win - base) // LANES)
+    for head in range(heads):
+        near_top, far_top = top[:, head : head + 1], stats[:, head : head + 1]
+        best = jnp.maximum(near_top, far_top)
+        near_part = jnp.exp2((near_top - best) * factor)
+        far_part = jnp.exp2((far_top - best) * factor)
+        far_sum = stats[:, heads + head : heads + head + 1]
+        inverse = 1.0 / (total[:, head : head + 1] * near_part + far_sum * far_part)
+        start, stop, own = window(width_win + head * head_dim, head_dim)
+        here = slice(start - base, stop - base)
+        near_share = acc[:, here] * jnp.where(own, near_part * inverse, 0.0)
+        far_share = message[:, here].astype(jnp.float32) * jnp.where(own, far_part * inverse, 0.0)
+        share = near_share + far_share
         for tile in range((stop - start) // LANES):
             at = (start - base) // LANES + tile
             piece = share[:, tile * LANES : (tile + 1) * LANES]
             tiles[at] = piece if tiles[at] is None else tiles[at] + piece
-        scores = later
     return jnp.concatenate(tiles, axis=1).astype(jnp.bfloat16)
 
 
@@ -170,8 +203,8 @@
 
 def block_kernel(
     head_dim, tokens_hbm, stale_hbm, spatial_w_hbm, spatial_o_hbm, temporal_w_hbm, temporal_o_hbm,
-    mod_ref, out_ref, tokens, kv0, kv1, kv2, kv3, q, spatial_w, spatial_o, temporal_w, temporal_o,
-    acc, top, total, leaving, arriving, mixed_out, mixed_in, load_sem, kv_send, kv_recv, in_send,
+    mod_ref, out_ref, tokens, kv0, kv1, stale, q, q_in, far_out, far_in, spatial_w, spatial_o, temporal_w, temporal_o,
+    acc, top, total, leaving, arriving, mixed_out, mixed_in, load_sem, kv_send, kv_recv, far_send, far_recv, in_send,
     in_recv, back_send, back_recv, own_sem,
 ):
     chunks, frames, pixels, _ = leaving.shape
@@ -195,6 +228,7 @@
             [
                 (tokens_hbm, tokens),
                 (spatial_w_hbm, spatial_w),
+                (stale_hbm, stale),
                 (spatial_o_hbm, spatial_o.at[width_win - base :]),
                 (temporal_w_hbm, temporal_w),
                 (temporal_o_hbm, temporal_o),
@@ -218,11 +252,14 @@
             device_id={"patch": other}, device_id_type=pl.DeviceIdType.MESH,
         )
 
-    across = remote(stale_hbm, kv2, kv_send.at[0], kv_recv.at[0], flip(2))
-    beside = remote(stale_hbm, kv1, kv_send.at[1], kv_recv.at[1], flip(1))
-    onward = remote(kv2, kv3, kv_send.at[2], kv_recv.at[2], flip(1))
-    across.start()
+    beside = remote(stale_hbm, kv1, kv_send.at[0], kv_recv.at[0], flip(1))
     beside.start()
+
+    def ask(c):
+        return remote(q.at[c], q_in.at[c], far_send.at[0, c], far_recv.at[0, c], flip(2))
+
+    def answer(c):
+        return remote(far_out.at[c], far_in.at[c], far_send.at[1, c], far_recv.at[1, c], flip(2))
 
     spatial_o[: width_win - base] = jnp.zeros((width_win - base, spatial_o.shape[1]), jnp.bfloat16)
     loads[0].wait()
@@ -241,26 +278,18 @@
         q[c, :, width_win:] = jnp.zeros((rows, q.shape[2] - width_win), jnp.bfloat16)
         kv0[here, :width_win] = fresh_k
         kv0[here, width_win:] = fresh_v
+        ask(c).start()
         return carry
 
     lax.fori_loop(0, chunks, project, 0)
+    for load in loads[2:]:
+        load.wait()
     beside.wait_recv()
 
-    near_count = 2 if chunks % 2 == 0 and rows <= 128 else 1
-
-    def near(block, carry):
-        at = block * near_count
-        q_rows = q[pl.ds(at, near_count)].reshape(near_count * rows, q.shape[2])
-        near_rows(head_dim, width_win, q_rows, (kv0, kv1), acc, top, total, at, near_count)
-        return carry
-
-    lax.fori_loop(0, chunks // near_count, near, 0)
-    across.wait_recv()
-    onward.start()
-    loads[2].wait()
-    loads[3].wait()
-    loads[4].wait()
-    onward.wait_recv()
+    def serve(c):
+        ask(c).wait_recv()
+        far_out[c] = far_message(head_dim, width_win, q_in[c], (stale, kv1))
+        answer(c).start()
 
     def inward(c, step):
         other, target = peer(step)
@@ -282,10 +311,10 @@
     def keep_back(c):
         return pltpu.make_async_copy(mixed_out.at[c, slot], mixed_in.at[c, slot], own_sem.at[1, c])
 
-    def far(c):
-        mixed = far_rows(
-            head_dim, width_win, q[c], (kv2, kv3), acc.at[c], top.at[c], total.at[c]
-        )
+    def own(c):
+        near_rows(head_dim, width_win, q[c], (kv0, kv1), acc, top, total, c, 1)
+        answer(c).wait_recv()
+        mixed = join(head_dim, width_win, far_in[c], acc.at[c], top.at[c], total.at[c])
         after, temporal_in = spatial_finish(
             mixed, tokens[c], spatial_o[...], mod_ref, mod_ref[6:7]
         )
@@ -306,19 +335,19 @@
             backward(c, step).start()
         keep_back(c).start()
 
-    lag = min(2, chunks - 1)
-
-    def first(c, carry):
-        far(c)
-
-        @pl.when(c >= lag)
+    def stage(k, carry):
+        @pl.when(k < chunks)
         def _():
-            temporal(c - lag)
-
-        return carry
-
-    def second(c, carry):
-        temporal(c)
+            serve(k)
+
+        @pl.when((k >= 1) & (k <= chunks))
+        def _():
+            own(k - 1)
+
+        @pl.when(k >= 2)
+        def _():
+            temporal(k - 2)
+
         return carry
 
     def third(c, carry):
@@ -330,19 +359,19 @@
         out_ref[c] = out_ref[c] + mod_ref[5:6] * projected
         return carry
 
-    lax.fori_loop(0, chunks, first, 0)
-    lax.fori_loop(chunks - lag, chunks, second, 0)
+    lax.fori_loop(0, chunks + 2, stage, 0)
     lax.fori_loop(0, chunks, third, 0)
 
     def drain(c, carry):
+        ask(c).wait_send()
+        answer(c).wait_send()
         for step in range(1, frames):
             inward(c, step)[1].wait_send()
             backward(c, step).wait_send()
         return carry
 
     lax.fori_loop(0, chunks, drain, 0)
-    for copy in (across, beside, onward):
-        copy.wait_send()
+    beside.wait_send()
 
 
 def per_device(
@@ -391,8 +420,10 @@
             pltpu.VMEM(flat, bf16),
             pltpu.VMEM(flat, bf16),
             pltpu.VMEM(flat, bf16),
-            pltpu.VMEM(flat, bf16),
             pltpu.VMEM((chunks, rows, q_width), bf16),
+            pltpu.VMEM((chunks, rows, q_width), bf16),
+            pltpu.VMEM((chunks, rows, v_width), bf16),
+            pltpu.VMEM((chunks, rows, v_width), bf16),
             pltpu.VMEM((3 * width_win, feature_width), bf16),
             pltpu.VMEM((v_width, feature_width), bf16),
             pltpu.VMEM((3 * width_win, feature_width), bf16),
@@ -404,9 +435,11 @@
             pltpu.VMEM(exchanged + (feature_width,), bf16),
             pltpu.VMEM(exchanged + (width_win,), bf16),
             pltpu.VMEM(exchanged + (width_win,), bf16),
-            pltpu.SemaphoreType.DMA((5,)),
-            pltpu.SemaphoreType.DMA((3,)),
-            pltpu.SemaphoreType.DMA((3,)),
+            pltpu.SemaphoreType.DMA((6,)),
+            pltpu.SemaphoreType.DMA((1,)),
+            pltpu.SemaphoreType.DMA((1,)),
+            pltpu.SemaphoreType.DMA((2, chunks)),
+            pltpu.SemaphoreType.DMA((2, chunks)),
             pltpu.SemaphoreType.DMA((chunks, frames)),
             pltpu.SemaphoreType.DMA((chunks, frames)),
             pltpu.SemaphoreType.DMA((chunks, frames)),

time: 90.1 us -> 81.7 us (0.907)
  Pallas kernels: 81.6 us -> 73.7 us
    pallas_call x1, Pallas kernels: 81.6 us -> 73.7 us  [per_device(): pl.pallas_call(functools.partial(block_kernel, head_dim), in_specs=[anywh...]
where the time goes in v3:
time: 81.7 us; the launch traced here: 81.4 us
  Pallas kernels  73.7 us (90%)
  local copies, waits for them, and re-layouts  3.3 us (4%)
  other arithmetic  3.04 us (4%)
  between operations  1.33 us (2%)
    pallas_call x1, Pallas kernels, per_device(): pl.pallas_call(functools.partial(block_kernel, head_dim), in_specs=[anywh...  73.7 us
    unnamed x1, local copies, waits for them, and re-layouts  3.22 us

profile of v3, /device:TPU:0, one launch (start us, length us, event | category | flops | bytes accessed | tf_op | source)
XLA Modules:
  0.0 81.4 jit_solution(4406616096205816169)
XLA Ops:
  0.7 1.3 %fusion.6 = s32[]{:T(128)} fusion(s32[4]{0:T(128)} %param.15, s32[]{:T(128)S(6)} %select_n.9), kind=kLoop, calls=%fused_computation.12 | loop fusion | flops 11 | bytes 24 | tf_op jit(solution)/shard_map/reduce_sum | solution.py:401
  2.6 0.1 pad.2.clone
  2.7 0.1 pad_maximum_fusion.1
  2.8 0.1 fusion.2
  2.9 0.1 pad_maximum_fusion
  2.9 0.8 multiply_add_fusion
  3.8 0.7 maximum_maximum_fusion.mod_ref
  4.4 73.7 %denoising_block.1 = f32[4,128,1152]{2,1,0:T(8,128)} custom-call(bf16[4,128,1152]{2,1,0:T(8,128)(2,1)} %bitcast.13, bf16[512,1152]{1,0:T(8,128)(2,1)} %stale_hbm.1, bf16[1728,1152]{1,0:T(8,128)(2,1)} %bitcast.11, bf16[576,1152]{1,0:T(8,128)(2,1)} %spatial_o_hbm.1, bf16[1728,1152]{1,0:T(8,128)(2,1)} %bitcast.12, bf16[576,1152]{1,0:T(8,128)(2,1)} %temporal_o_hbm.1, ...), custom_call_target="tpu_custom_call" | custom-call | tf_op jit(solution)/shard_map/denoising_block/pallas_call | solution.py:413
  78.1 3.2 %copy.13 = f32[512,1152]{1,0:T(8,128)} copy(f32[512,1152]{1,0:T(8,128)} %bitcast.10) | data formatting | bytes 4718592
  (2 shorter events, 0.1 us)
